TPU v7x, 256 devices: a whole 4x4x8 slice. The times are simulated.
256 devices in a mesh: rep: 8 (over x_lo, y), tp: 8 (over z), fs: 4 (over x_hi, core).
Axes of the slice: x: 4 (x_hi: 2, x_lo: 2; x = x_hi * 2 + x_lo), y: 4, z: 8, core: 2. Of those that a mesh axis runs over, the one named last changes fastest.
Arguments:
- hidden: bfloat16 [64, 8192], P(('rep', 'fs'), 'tp'), may hold values from -6 to 6
- cache_key: bfloat16 [64, 2048, 1024], P(('rep', 'fs'), None, 'tp'), may hold values from -1300 to 1300
- cache_value: bfloat16 [64, 2048, 1024], P(('rep', 'fs'), None, 'tp'), may hold values from -6 to 6
- lengths: int32 [64], P(('rep', 'fs')), may hold values from 8 to 2047
- owner: int32 [1], replicated, may hold values from 0 to 32767
- query_weight: bfloat16 [8, 8192, 4096], P('rep', 'fs', 'tp'), may hold values from -0.0625 to 0.0625
- key_weight: bfloat16 [8, 8192, 1024], P('rep', 'fs', 'tp'), may hold values from -0.0625 to 0.0625
- value_weight: bfloat16 [8, 8192, 1024], P('rep', 'fs', 'tp'), may hold values from -0.0625 to 0.0625
- out_weight: bfloat16 [8, 4096, 8192], P('rep', 'tp', 'fs'), may hold values from -0.09375 to 0.09375
Outputs:
- mixed: bfloat16 [64, 8192], P(('rep', 'fs'), 'tp')
- new_key: bfloat16 [64, 1024], P(('rep', 'fs'), 'tp')
- new_value: bfloat16 [64, 1024], P(('rep', 'fs'), 'tp')
- fresh_query: bfloat16 [8, 8192, 4096], P('rep', 'fs', 'tp')
- fresh_key: bfloat16 [8, 8192, 1024], P('rep', 'fs', 'tp')
- fresh_value: bfloat16 [8, 8192, 1024], P('rep', 'fs', 'tp')
- fresh_out: bfloat16 [8, 4096, 8192], P('rep', 'tp', 'fs')
Inputs may be any that keep to these rules, and one draw needn't show every extreme that they name: `lengths`: the number of positions already in each sequence's cache; the new token stands at that position.
All inputs are finite; a program needn't handle non-finite values.
Results may differ from a plain program's by a relative error of at most 0.0065.
Values may be sent and summed in bfloat16 or wider, within the bound.
No kernel may reach another device: no remote copies, remote signals or barrier semaphores. Data moves between devices by JAX's collectives and lax.ppermute only.
A program may use at most 64 MiB of HBM per device.

v0:
```python
import jax
import jax.numpy as jnp
from jax import lax
from jax.sharding import PartitionSpec as P

DH = 128
rope_base = 500000.0
epsilon = 1e-05


def from_root(shard, axis, root):
    mine = lax.axis_index(axis) == root
    return lax.psum(jnp.where(mine, shard, jnp.zeros_like(shard)), axis)


def cut_along(shard, dim, peers):
    lengths = shard.shape
    parts = shard.reshape(*lengths[:dim], peers, lengths[dim] // peers, *lengths[dim + 1 :])
    return jnp.moveaxis(parts, dim, 0)


def sent_and_summed(shard, axis, dim):
    peers = lax.axis_size(axis)
    parts = lax.all_to_all(cut_along(shard, dim, peers), axis, 0, 0, tiled=True)
    return jnp.sum(parts, axis=0)


def copy_for_each(shard, axis):
    peers = lax.axis_size(axis)
    return lax.all_to_all(
        jnp.broadcast_to(shard[None], (peers, *shard.shape)), axis, 0, 0, tiled=True
    )


def joined_along(parts, dim):
    parts = jnp.moveaxis(parts, 0, dim)
    lengths = parts.shape
    return parts.reshape(*lengths[:dim], lengths[dim] * lengths[dim + 1], *lengths[dim + 2 :])


def collect(shard, axis, dim):
    parts = copy_for_each(shard, axis)
    return joined_along(parts, dim)


def rotate(heads, positions):
    half_dim = heads.shape[-1] // 2
    frequency = rope_base ** (-(jnp.arange(half_dim, dtype=jnp.float32) * 2.0 / heads.shape[-1]))
    angles = positions.astype(jnp.float32)[:, None] * frequency[None, :]
    cosine = jnp.cos(angles)[:, None, :]
    sine_part = jnp.sin(angles)[:, None, :]
    first_half = heads[..., :half_dim]
    second_half = heads[..., half_dim:]
    return jnp.concatenate(
        [
            first_half * cosine - second_half * sine_part,
            second_half * cosine + first_half * sine_part,
        ],
        axis=-1,
    )


def attend(query, own_key, own_value, cache_key, cache_value, lengths):
    seqs, span, width = cache_key.shape
    kv_local = query.shape[1]
    head_size = query.shape[3]
    keys_view = cache_key.reshape(seqs, span, kv_local, head_size)
    values_view = cache_value.reshape(seqs, span, kv_local, head_size)
    scale = head_size ** (-0.5)
    scores = (
        jnp.einsum("shgd,sthd->shgt", query, keys_view, preferred_element_type=jnp.float32) * scale
    )
    own_score = (
        jnp.einsum("shgd,shd->shg", query, own_key, preferred_element_type=jnp.float32) * scale
    )
    live = (jnp.arange(span, dtype=jnp.int32)[None, :] < lengths[:, None])[:, None, None, :]
    masked = jnp.where(live, scores, -jnp.inf)
    row_max = jnp.maximum(jnp.max(masked, axis=-1), own_score)
    weights = jnp.where(live, jnp.exp(scores - row_max[..., None]), 0.0)
    own_weight = jnp.exp(own_score - row_max)
    denominator = jnp.sum(weights, axis=-1) + own_weight
    probs = (weights / denominator[..., None]).astype(jnp.bfloat16)
    own_prob = (own_weight / denominator).astype(jnp.bfloat16)
    context = jnp.einsum("shgt,sthd->shgd", probs, values_view, preferred_element_type=jnp.float32)
    return (
        context
        + own_prob.astype(jnp.float32)[..., None] * own_value.astype(jnp.float32)[:, :, None, :]
    )


def from_owner(parts, owner_rank):
    peers = lax.axis_size("rep")
    grouped = parts.reshape(peers, parts.shape[0] // peers, *parts.shape[1:])
    return lax.dynamic_index_in_dim(grouped, owner_rank, 0, keepdims=False)


def local(
    hidden,
    cache_key,
    cache_value,
    lengths,
    owner,
    query_weight,
    key_weight,
    value_weight,
    out_weight,
):
    reps, fss, tps = (lax.axis_size("rep"), lax.axis_size("fs"), lax.axis_size("tp"))
    owner_rank = owner[0] % reps
    fresh_query, fresh_key, fresh_value, fresh_out = (
        from_root(query_weight, "rep", owner_rank),
        from_root(key_weight, "rep", owner_rank),
        from_root(value_weight, "rep", owner_rank),
        from_root(out_weight, "rep", owner_rank),
    )
    seqs = hidden.shape[0]
    hidden_wide = collect(hidden, "tp", 1).astype(jnp.float32)
    normed = (
        hidden_wide
        * lax.rsqrt(jnp.mean(hidden_wide * hidden_wide, axis=-1, keepdims=True) + epsilon)
    ).astype(jnp.bfloat16)
    blocks = cut_along(normed, 1, fss)
    blocks = jnp.broadcast_to(blocks[None], (reps, *blocks.shape))
    blocks = blocks.reshape(reps * fss, *blocks.shape[2:])
    tokens = lax.all_to_all(blocks, ("rep", "fs"), 0, 0, tiled=True)
    tokens = tokens.reshape(reps * fss * seqs, tokens.shape[-1])
    query_width = query_weight.shape[2]
    key_width = key_weight.shape[2]
    partial = jnp.concatenate(
        [
            jnp.dot(tokens, query_weight[0], preferred_element_type=jnp.float32),
            jnp.dot(tokens, key_weight[0], preferred_element_type=jnp.float32),
            jnp.dot(tokens, value_weight[0], preferred_element_type=jnp.float32),
        ],
        axis=1,
    )
    partial = partial.reshape(reps * fss, seqs, partial.shape[1])
    shares = lax.all_to_all(partial, ("rep", "fs"), 0, 0, tiled=True)
    joined = jnp.sum(from_owner(shares, owner_rank), axis=0)
    query_proj = joined[:, :query_width]
    key_proj = joined[:, query_width : query_width + key_width]
    value_proj = joined[:, query_width + key_width :]
    q_heads = query_proj.shape[1] // DH
    kv_heads = key_proj.shape[1] // DH
    query_rot = rotate(query_proj.reshape(seqs, q_heads, DH), lengths).astype(jnp.bfloat16)
    query_rot = query_rot.reshape(seqs, kv_heads, q_heads // kv_heads, DH)
    key_new = rotate(key_proj.reshape(seqs, kv_heads, DH), lengths).astype(jnp.bfloat16)
    value_new = value_proj.astype(jnp.bfloat16).reshape(seqs, kv_heads, DH)
    context = attend(query_rot, key_new, value_new, cache_key, cache_value, lengths)
    context = context.astype(jnp.bfloat16).reshape(seqs, q_heads * DH)
    contexts = lax.all_to_all(
        jnp.broadcast_to(context[None], (reps * fss, *context.shape)),
        ("rep", "fs"),
        0,
        0,
        tiled=True,
    ).reshape(reps * fss * seqs, q_heads * DH)
    partial_out = jnp.dot(contexts, out_weight[0], preferred_element_type=jnp.float32)
    partial_out = partial_out.reshape(reps * fss, seqs, partial_out.shape[1])
    terms = lax.all_to_all(partial_out, ("rep", "fs"), 0, 0, tiled=True)
    terms = joined_along(from_owner(terms, owner_rank), 1)
    summed = sent_and_summed(terms, "tp", 1)
    mixed = (summed + hidden.astype(jnp.float32)).astype(jnp.bfloat16)
    return (
        mixed,
        key_new.reshape(seqs, kv_heads * DH),
        value_new.reshape(seqs, kv_heads * DH),
        fresh_query,
        fresh_key,
        fresh_value,
        fresh_out,
    )


def solution(mesh):
    return jax.shard_map(
        local,
        mesh=mesh,
        in_specs=(
            P(("rep", "fs"), "tp"),
            P(("rep", "fs"), None, "tp"),
            P(("rep", "fs"), None, "tp"),
            P(("rep", "fs")),
            P(),
            P("rep", "fs", "tp"),
            P("rep", "fs", "tp"),
            P("rep", "fs", "tp"),
            P("rep", "tp", "fs"),
        ),
        out_specs=(
            P(("rep", "fs"), "tp"),
            P(("rep", "fs"), "tp"),
            P(("rep", "fs"), "tp"),
            P("rep", "fs", "tp"),
            P("rep", "fs", "tp"),
            P("rep", "fs", "tp"),
            P("rep", "tp", "fs"),
        ),
        check_vma=False,
    )
```

profile of v0, /device:TPU:1, one launch (start us, length us, event | category | flops | bytes accessed | tf_op | source)
XLA Modules:
  0.0 176.9 jit_solution(9229973164668991891)
XLA Ops:
  7.2 1.4 broadcast_in_dim.31
  8.6 9.0 %all-to-all-start = ((bf16[8,2,1024]{2,1,0:T(2,128)(2,1)}), bf16[8,2,1024]{2,1,0:T(2,128)(2,1)S(1)}, u32[]{:S(2)}, u32[]{:S(2)}) async-start(bf16[8,2,1024]{2,1,0:T(2,128)(2,1)} %broadcast_in_dim.31), calls=%async_computation | async-start | bytes 65536 | tf_op jit(solution)/shard_map/all_to_all | solution.py:30
  18.3 1.5 broadcast_select_fusion
  19.8 0.9 copy-done.1
  20.6 1.5 broadcast_select_fusion.1
  22.2 1.0 broadcast_select_fusion.2
  23.3 1.2 all-to-all-done
  24.9 0.9 broadcast_in_dim.32
  25.8 9.2 %all-to-all-start.1 = ((bf16[32,2,2048]{2,1,0:T(2,128)(2,1)}), bf16[32,2,2048]{2,1,0:T(2,128)(2,1)}, u32[]{:S(2)}, u32[]{:S(2)}) async-start(bf16[32,2,2048]{2,1,0:T(2,128)(2,1)} %bitcast.2), calls=%async_computation.1 | async-start | bytes 524288 | tf_op jit(solution)/shard_map/all_to_all | solution.py:125
  35.2 9.0 %all-to-all-done.1 = bf16[32,2,2048]{2,1,0:T(2,128)(2,1)} async-done(((bf16[32,2,2048]{2,1,0:T(2,128)(2,1)}), bf16[32,2,2048]{2,1,0:T(2,128)(2,1)}, u32[]{:S(2)}, u32[]{:S(2)}) %all-to-all-start.1) | async-done | bytes 262176 | tf_op jit(solution)/shard_map/all_to_all | solution.py:125
  44.2 1.0 reshape.261
  45.2 1.3 fusion.6
  46.5 1.3 fusion.8
  47.8 0.5 fusion.2
  48.3 0.8 reshape.262
  49.1 5.5 %all-to-all-start.2 = ((f32[32,2,768]{2,1,0:T(2,128)}), f32[32,2,768]{2,1,0:T(2,128)S(1)}, u32[]{:S(2)}, u32[]{:S(2)}) async-start(f32[32,2,768]{2,1,0:T(2,128)} %reshape.262), calls=%async_computation.2 | async-start | bytes 393216 | tf_op jit(solution)/shard_map/all_to_all | solution.py:138
  54.7 9.4 %all-to-all-done.2 = f32[32,2,768]{2,1,0:T(2,128)S(1)} async-done(((f32[32,2,768]{2,1,0:T(2,128)}), f32[32,2,768]{2,1,0:T(2,128)S(1)}, u32[]{:S(2)}, u32[]{:S(2)}) %all-to-all-start.2) | async-done | bytes 196640 | tf_op jit(solution)/shard_map/all_to_all | solution.py:138
  64.2 0.5 fusion.33
  65.0 0.5 select_reduce_fusion
  65.6 0.2 fusion.12
  65.8 1.5 fusion.5
  67.4 40.5 %all_to_all.30 = bf16[32,2,512]{2,1,0:T(2,128)(2,1)S(1)} all-to-all(bf16[32,2,512]{2,1,0:T(2,128)(2,1)S(1)} %broadcast_in_dim.36), channel_id=1, replica_groups=mesh['rep'=8,'tp'=8,'fs'=4] {'rep','fs'}, dimensions={0} | all-to-all | bytes 131072 | tf_op jit(solution)/shard_map/all_to_all | solution.py:151
  107.9 0.5 fusion
  108.4 0.4 copy.21
  108.8 18.9 %all_to_all.31 = f32[32,2,2048]{2,1,0:T(2,128)S(1)} all-to-all(f32[32,2,2048]{2,1,0:T(2,128)S(1)} %copy.21), channel_id=1, replica_groups=mesh['rep'=8,'tp'=8,'fs'=4] {'rep','fs'}, dimensions={0} | all-to-all | bytes 1048576 | tf_op jit(solution)/shard_map/all_to_all | solution.py:160
  127.7 12.1 %all_to_all.32 = f32[8,2,1024]{2,1,0:T(2,128)S(1)} all-to-all(f32[8,2,1024]{2,1,0:T(2,128)S(1)} %bitcast.51), channel_id=1, replica_groups=mesh['rep'=8,'tp'=8,'fs'=4] {'tp'}, dimensions={0} | all-to-all | bytes 131072 | tf_op jit(solution)/shard_map/all_to_all | solution.py:24
  139.8 0.6 add_convert_fusion
  140.4 23.6 %all-reduce.3.cloned.1.call-done = (bf16[1,2048,512]{2,1,0:T(8,128)(2,1)}, bf16[1,2048,128]{2,1,0:T(8,128)(2,1)}, bf16[1,2048,128]{2,1,0:T(8,128)(2,1)}, bf16[1,512,2048]{2,1,0:T(8,128)(2,1)}) async-done(((bf16[1,2048,512]{2,1,0:T(8,128)(2,1)}, bf16[1,2048,128]{2,1,0:T(8,128)(2,1)}, bf16[1,2048,128]{2,1,0:T(8,128)(2,1)}, bf16[1,512,2048]{2,1,0:T(8,128)(2,1)}), (bf16[1,2048,512]{2,1,0:T(8,128)(2,1)}, ...) | async-done | bytes 5242896 | tf_op jit(solution)/shard_map/psum | solution.py:13
  164.0 3.2 %copy.36 = bf16[1,2048,512]{2,1,0:T(8,128)(2,1)} copy(bf16[1,2048,512]{2,1,0:T(8,128)(2,1)} %get-tuple-element.29) | data formatting | bytes 4194304
  167.2 0.8 copy.37
  168.0 0.8 copy.38
  168.8 1.3 copy.39
  (48 shorter events, 1.4 us)
Async XLA Ops:
  7.2 57.9 %copy-start = (bf16[2,2048,128]{2,1,0:T(8,128)(2,1)S(1)}, bf16[2,2048,128]{2,1,0:T(8,128)(2,1)}, u32[]{:S(2)}) copy-start(bf16[2,2048,128]{2,1,0:T(8,128)(2,1)} %param.10) | copy-start | bytes 3145732
  8.6 15.9 %all-to-all-start = ((bf16[8,2,1024]{2,1,0:T(2,128)(2,1)}), bf16[8,2,1024]{2,1,0:T(2,128)(2,1)S(1)}, u32[]{:S(2)}, u32[]{:S(2)}) async-start(bf16[8,2,1024]{2,1,0:T(2,128)(2,1)} %broadcast_in_dim.31), calls=%async_computation | async-start | bytes 65536 | tf_op jit(solution)/shard_map/all_to_all | solution.py:30
  17.6 146.4 %all-reduce.3.cloned.1.call-start = ((), (), s32[]{:S(2)}) async-start(), calls=%async_computation.6 | async-start | bytes 10485760 | tf_op jit(solution)/shard_map/psum | solution.py:13
  18.3 2.4 %copy-start.1 = (bf16[1,2048,512]{2,1,0:T(8,128)(2,1)S(1)}, bf16[1,2048,512]{2,1,0:T(8,128)(2,1)}, u32[]{:S(2)}) copy-start(bf16[1,2048,512]{2,1,0:T(8,128)(2,1)} %param.14) | copy-start | bytes 6291460
  20.6 1.5 copy-start.3
  20.6 1.6 copy-start.4
  23.3 11.8 %copy-start.9 = (s32[2]{0:T(128)S(1)}, s32[2]{0:T(128)}, u32[]{:S(2)}) copy-start(s32[2]{0:T(128)} %param.12) | copy-start | bytes 28
  25.8 18.4 %all-to-all-start.1 = ((bf16[32,2,2048]{2,1,0:T(2,128)(2,1)}), bf16[32,2,2048]{2,1,0:T(2,128)(2,1)}, u32[]{:S(2)}, u32[]{:S(2)}) async-start(bf16[32,2,2048]{2,1,0:T(2,128)(2,1)} %bitcast.2), calls=%async_computation.1 | async-start | bytes 524288 | tf_op jit(solution)/shard_map/all_to_all | solution.py:125
  48.2 59.6 %copy-start.2 = (bf16[1,512,2048]{2,1,0:T(8,128)(2,1)S(1)}, bf16[1,512,2048]{2,1,0:T(8,128)(2,1)}, u32[]{:S(2)}) copy-start(bf16[1,512,2048]{2,1,0:T(8,128)(2,1)} %param.17) | copy-start | bytes 6291460
  49.1 15.0 %all-to-all-start.2 = ((f32[32,2,768]{2,1,0:T(2,128)}), f32[32,2,768]{2,1,0:T(2,128)S(1)}, u32[]{:S(2)}, u32[]{:S(2)}) async-start(f32[32,2,768]{2,1,0:T(2,128)} %reshape.262), calls=%async_computation.2 | async-start | bytes 393216 | tf_op jit(solution)/shard_map/all_to_all | solution.py:138
  64.8 43.6 %copy-start.10 = (bf16[2,128]{1,0:T(2,128)(2,1)}, bf16[2,128]{1,0:T(2,128)(2,1)S(1)}, u32[]{:S(2)}) copy-start(bf16[2,128]{1,0:T(2,128)(2,1)S(1)} %get-tuple-element.27) | copy-start | bytes 1540
  107.9 31.9 %copy-start.8 = (bf16[2,1024]{1,0:T(2,128)(2,1)S(1)}, bf16[2,1024]{1,0:T(2,128)(2,1)}, u32[]{:S(2)}) copy-start(bf16[2,1024]{1,0:T(2,128)(2,1)} %param.9) | copy-start | bytes 12292
  164.0 3.2 %copy-start.7 = (bf16[1,2048,128]{2,1,0:T(8,128)(2,1)S(1)}, bf16[1,2048,128]{2,1,0:T(8,128)(2,1)}, u32[]{:S(2)}) copy-start(bf16[1,2048,128]{2,1,0:T(8,128)(2,1)} %get-tuple-element.30) | copy-start | bytes 1572868
  164.0 4.0 %copy-start.6 = (bf16[1,2048,128]{2,1,0:T(8,128)(2,1)S(1)}, bf16[1,2048,128]{2,1,0:T(8,128)(2,1)}, u32[]{:S(2)}) copy-start(bf16[1,2048,128]{2,1,0:T(8,128)(2,1)} %get-tuple-element.31) | copy-start | bytes 1572868
  164.0 4.8 %copy-start.5 = (bf16[1,512,2048]{2,1,0:T(8,128)(2,1)S(1)}, bf16[1,512,2048]{2,1,0:T(8,128)(2,1)}, u32[]{:S(2)}) copy-start(bf16[1,512,2048]{2,1,0:T(8,128)(2,1)} %get-tuple-element.32) | copy-start | bytes 6291460
Sparse Core Ops, SparseCore 0:
  23.4 140.5 all-reduce.2
where the time goes:
time: 178 us; the launch traced here: 177 us
  blocking collectives  71.5 us (40%)
  waiting for transfers between devices  43.2 us (24%)
  starting transfers between devices  23.7 us (13%)
  between operations  14.9 us (8%)
  local copies, waits for them, and re-layouts  11.8 us (7%)
  other arithmetic  6.06 us (3%)
  matrix products  5.73 us (3%)
    all_to_all x1, blocking collectives, local(): lax.all_to_all(jnp.broadcast_to(context[None], (reps * fss, *context.shap...  40.5 us
    psum x1, waiting for transfers between devices, from_root(): return lax.psum(jnp.where(mine, shard, jnp.zeros_like(shard)), axis)  23.6 us
    all_to_all x1, blocking collectives, local(): terms = lax.all_to_all(partial_out, ('rep', 'fs'), 0, 0, tiled=True)  18.9 us
    all_to_all x1, blocking collectives, sent_and_summed(): parts = lax.all_to_all(cut_along(shard, dim, peers), axis, 0, 0, tiled=True)  12.1 us
    all_to_all x1, waiting for transfers between devices, local(): shares = lax.all_to_all(partial, ('rep', 'fs'), 0, 0, tiled=True)  9.43 us
    all_to_all x1, starting transfers between devices, local(): tokens = lax.all_to_all(blocks, ('rep', 'fs'), 0, 0, tiled=True)  9.25 us
    all_to_all x1, waiting for transfers between devices, local(): tokens = lax.all_to_all(blocks, ('rep', 'fs'), 0, 0, tiled=True)  9.01 us
    all_to_all x1, starting transfers between devices, copy_for_each(): lax.all_to_all(jnp.broadcast_to(shard[None], (peers, *shard.shape)), axis...  9 us
  transfers between devices with their start and end apart: 4, of which 4 were waited for; matrix products, arithmetic and copies ran while one was open for 9% of the time, Pallas kernels for 0%

commit v1 on v0

--- a/solution.py
+++ b/solution.py
@@ -10,7 +10,7 @@
 
 def from_root(shard, axis, root):
     mine = lax.axis_index(axis) == root
-    return lax.psum(jnp.where(mine, shard, jnp.zeros_like(shard)), axis)
+    return jnp.sum(lax.all_gather(jnp.where(mine, shard, jnp.zeros_like(shard)), axis), axis=0)
 
 
 def cut_along(shard, dim, peers):

time: 178 us -> 501 us (2.81)
  waiting for transfers between devices: 43.2 us -> 370 us
  other arithmetic: 6.06 us -> 35.4 us
  blocking collectives: 71.5 us -> 55.9 us
  starting transfers between devices: 23.7 us -> 15 us
  local copies, waits for them, and re-layouts: 11.8 us -> 4 us
    all_gather x0 -> x4, waiting for transfers between devices: none -> 349 us  [from_root(): lax.all_gather(jnp.where(mine, shard, jnp.zeros_like(shard)), axis)]
    all_to_all x1, blocking collectives: 40.5 us -> 11.7 us  [local(): lax.all_to_all(jnp.broadcast_to(context[None], (reps * fss, *context.shap...]
    reduce_sum x0 -> x4, other arithmetic: none -> 28.7 us  [from_root(): jnp.sum(lax.all_gather(jnp.where(mine, shard, jnp.zeros_like(shard)), axi...]
    psum x1 -> x0, waiting for transfers between devices: 23.6 us -> none  [from_root(): return lax.psum(jnp.where(mine, shard, jnp.zeros_like(shard)), axis)]
    all_to_all x0 -> x1, blocking collectives: none -> 15.7 us  [copy_for_each(): lax.all_to_all(jnp.broadcast_to(shard[None], (peers, *shard.shape)), axis...]
    all_to_all x1 -> x0, starting transfers between devices: 9 us -> none  [copy_for_each(): lax.all_to_all(jnp.broadcast_to(shard[None], (peers, *shard.shape)), axis...]
    unnamed x27 -> x13, local copies, waits for them, and re-layouts: 7.14 us -> 0.69 us
  transfers between devices with their start and end apart: 4 -> 6, of which waited for: 4 -> 5; matrix products, arithmetic and copies ran while one was open for 9% -> 7% of each run, Pallas kernels for 0% -> 0%
where the time goes in v1:
time: 501 us; the launch traced here: 500 us
  waiting for transfers between devices  370 us (74%)
  blocking collectives  55.9 us (11%)
  other arithmetic  35.4 us (7%)
  starting transfers between devices  15 us (3%)
  between operations  14.8 us (3%)
  matrix products  5.73 us (1%)
    all_gather x4, waiting for transfers between devices, from_root(): lax.all_gather(jnp.where(mine, shard, jnp.zeros_like(shard)), axis)  349 us
    reduce_sum x4, other arithmetic, from_root(): jnp.sum(lax.all_gather(jnp.where(mine, shard, jnp.zeros_like(shard)), axi...  28.7 us
    all_to_all x1, blocking collectives, local(): terms = lax.all_to_all(partial_out, ('rep', 'fs'), 0, 0, tiled=True)  18.9 us
    all_to_all x1, blocking collectives, copy_for_each(): lax.all_to_all(jnp.broadcast_to(shard[None], (peers, *shard.shape)), axis...  15.7 us
    all_to_all x1, blocking collectives, local(): lax.all_to_all(jnp.broadcast_to(context[None], (reps * fss, *context.shap...  11.7 us
    all_to_all x1, waiting for transfers between devices, local(): tokens = lax.all_to_all(blocks, ('rep', 'fs'), 0, 0, tiled=True)  10.8 us
    all_to_all x1, starting transfers between devices, local(): tokens = lax.all_to_all(blocks, ('rep', 'fs'), 0, 0, tiled=True)  10.1 us
  transfers between devices with their start and end apart: 6, of which 5 were waited for; matrix products, arithmetic and copies ran while one was open for 7% of the time, Pallas kernels for 0%

profile of v1, /device:TPU:1, one launch (start us, length us, event | category | flops | bytes accessed | tf_op | source)
XLA Modules:
  0.0 500.4 jit_solution(17463418555093753886)
XLA Ops:
  8.1 0.8 broadcast_select_fusion.3
  9.0 0.8 broadcast_select_fusion.2
  9.9 1.5 broadcast_select_fusion.1
  11.4 1.5 broadcast_select_fusion
  12.9 0.7 copy-done.3
  13.6 15.7 %all_to_all.30 = bf16[8,2,1024]{2,1,0:T(2,128)(2,1)S(1)} all-to-all(bf16[8,2,1024]{2,1,0:T(2,128)(2,1)S(1)} %broadcast_in_dim.31), channel_id=1, replica_groups=mesh['rep'=8,'tp'=8,'fs'=4] {'tp'}, dimensions={0} | all-to-all | bytes 65536 | tf_op jit(solution)/shard_map/all_to_all | solution.py:30
  29.7 0.9 broadcast_in_dim.32
  30.6 10.1 %all-to-all-start.1 = ((bf16[32,2,2048]{2,1,0:T(2,128)(2,1)}), bf16[32,2,2048]{2,1,0:T(2,128)(2,1)}, u32[]{:S(2)}, u32[]{:S(2)}) async-start(bf16[32,2,2048]{2,1,0:T(2,128)(2,1)} %bitcast.2), calls=%async_computation.1 | async-start | bytes 524288 | tf_op jit(solution)/shard_map/all_to_all | solution.py:125
  40.8 10.8 %all-to-all-done.1 = bf16[32,2,2048]{2,1,0:T(2,128)(2,1)} async-done(((bf16[32,2,2048]{2,1,0:T(2,128)(2,1)}), bf16[32,2,2048]{2,1,0:T(2,128)(2,1)}, u32[]{:S(2)}, u32[]{:S(2)}) %all-to-all-start.1) | async-done | bytes 262176 | tf_op jit(solution)/shard_map/all_to_all | solution.py:125
  51.6 1.0 reshape.265
  52.7 1.3 fusion.6
  54.0 1.3 fusion.8
  55.2 0.5 fusion.2
  55.8 0.8 reshape.266
  56.5 4.7 all-to-all-start.2
  61.4 9.3 %all-to-all-done.2 = f32[32,2,768]{2,1,0:T(2,128)S(1)} async-done(((f32[32,2,768]{2,1,0:T(2,128)}), f32[32,2,768]{2,1,0:T(2,128)S(1)}, u32[]{:S(2)}, u32[]{:S(2)}) %all-to-all-start.2) | async-done | bytes 196640 | tf_op jit(solution)/shard_map/all_to_all | solution.py:138
  70.9 0.5 fusion.33
  71.7 0.5 select_reduce_fusion
  72.4 1.5 fusion.5
  74.0 11.7 %all_to_all.31 = bf16[32,2,512]{2,1,0:T(2,128)(2,1)S(1)} all-to-all(bf16[32,2,512]{2,1,0:T(2,128)(2,1)S(1)} %broadcast_in_dim.36), channel_id=1, replica_groups=mesh['rep'=8,'tp'=8,'fs'=4] {'rep','fs'}, dimensions={0} | all-to-all | bytes 131072 | tf_op jit(solution)/shard_map/all_to_all | solution.py:151
  85.8 0.5 fusion
  86.2 0.4 copy.21
  86.7 18.9 %all_to_all.32 = f32[32,2,2048]{2,1,0:T(2,128)S(1)} all-to-all(f32[32,2,2048]{2,1,0:T(2,128)S(1)} %copy.21), channel_id=1, replica_groups=mesh['rep'=8,'tp'=8,'fs'=4] {'rep','fs'}, dimensions={0} | all-to-all | bytes 1048576 | tf_op jit(solution)/shard_map/all_to_all | solution.py:160
  105.5 9.6 %all_to_all.33 = f32[8,2,1024]{2,1,0:T(2,128)S(1)} all-to-all(f32[8,2,1024]{2,1,0:T(2,128)S(1)} %bitcast.59), channel_id=1, replica_groups=mesh['rep'=8,'tp'=8,'fs'=4] {'tp'}, dimensions={0} | all-to-all | bytes 131072 | tf_op jit(solution)/shard_map/all_to_all | solution.py:24
  115.2 0.6 add_convert_fusion
  115.8 3.7 reduce.16
  119.5 17.2 %all-gather.13.cloned.1.call-done = bf16[8,2048,128]{2,1,0:T(8,128)(2,1)} async-done(((bf16[1,2048,128]{2,1,0:T(8,128)(2,1)}), bf16[8,2048,128]{2,1,0:T(8,128)(2,1)}) %all-gather.13.cloned.1.call-update) | async-done | bytes 4194320 | tf_op jit(solution)/shard_map/all_gather | solution.py:13
  136.7 3.7 reduce.17
  140.4 169.2 %all-gather.9.cloned.1.call-done = bf16[8,2048,512]{2,1,0:T(8,128)(2,1)} async-done(((bf16[1,2048,512]{2,1,0:T(8,128)(2,1)}), bf16[8,2048,512]{2,1,0:T(8,128)(2,1)}) %all-gather.9.cloned.1.call-update) | async-done | bytes 16777232 | tf_op jit(solution)/shard_map/all_gather | solution.py:13
  309.6 10.5 %reduce.15 = bf16[2048,512]{1,0:T(8,128)(2,1)} reduce(bf16[8,2048,512]{2,1,0:T(8,128)(2,1)} %all-gather.9.cloned.1.call-done, bf16[]{:T(256)} %constant.53.clone.1), dimensions={0}, to_apply=%region_5.6 | reduce | flops 7340032 | bytes 18874370 | tf_op jit(solution)/shard_map/reduce_sum | solution.py:13
  320.1 163.0 %all-gather.15.cloned.1.call-done = bf16[8,512,2048]{2,1,0:T(8,128)(2,1)} async-done(((bf16[1,512,2048]{2,1,0:T(8,128)(2,1)}), bf16[8,512,2048]{2,1,0:T(8,128)(2,1)}) %all-gather.15.cloned.1.call-update) | async-done | bytes 16777232 | tf_op jit(solution)/shard_map/all_gather | solution.py:13
  483.1 10.8 %reduce.18 = bf16[512,2048]{1,0:T(8,128)(2,1)} reduce(bf16[8,512,2048]{2,1,0:T(8,128)(2,1)} %all-gather.15.cloned.1.call-done, bf16[]{:T(256)} %constant.53.clone.1), dimensions={0}, to_apply=%region_8.9 | reduce | flops 7340032 | bytes 18874370 | tf_op jit(solution)/shard_map/reduce_sum | solution.py:13
  (47 shorter events, 1.6 us)
Async XLA Ops:
  7.2 64.5 %copy-start = (bf16[2,2048,128]{2,1,0:T(8,128)(2,1)S(1)}, bf16[2,2048,128]{2,1,0:T(8,128)(2,1)}, u32[]{:S(2)}) copy-start(bf16[2,2048,128]{2,1,0:T(8,128)(2,1)} %param.10) | copy-start | bytes 3145732
  7.2 2.7 copy-start.1
  7.2 108.6 %all-gather.11.cloned.1.call-start = ((), (), s32[]{:S(2)}) async-start(), calls=%async_computation.7 | async-start | bytes 4718592 | tf_op jit(solution)/shard_map/all_gather | solution.py:13
  8.9 127.8 %all-gather.13.cloned.1.call-start = ((), (), s32[]{:S(2)}) async-start(), calls=%async_computation.8 | async-start | bytes 4718592 | tf_op jit(solution)/shard_map/all_gather | solution.py:13
  9.8 299.7 %all-gather.9.cloned.1.call-start = ((), (), s32[]{:S(2)}) async-start(), calls=%async_computation.6 | async-start | bytes 18874368 | tf_op jit(solution)/shard_map/all_gather | solution.py:13
  11.4 471.7 %all-gather.15.cloned.1.call-start = ((), (), s32[]{:S(2)}) async-start(), calls=%async_computation.9 | async-start | bytes 18874368 | tf_op jit(solution)/shard_map/all_gather | solution.py:13
  12.9 0.7 copy-start.3
  12.9 27.8 %copy-start.4 = (s32[2]{0:T(128)S(1)}, s32[2]{0:T(128)}, u32[]{:S(2)}) copy-start(s32[2]{0:T(128)} %param.12) | copy-start | bytes 28
  30.6 21.0 %all-to-all-start.1 = ((bf16[32,2,2048]{2,1,0:T(2,128)(2,1)}), bf16[32,2,2048]{2,1,0:T(2,128)(2,1)}, u32[]{:S(2)}, u32[]{:S(2)}) async-start(bf16[32,2,2048]{2,1,0:T(2,128)(2,1)} %bitcast.2), calls=%async_computation.1 | async-start | bytes 524288 | tf_op jit(solution)/shard_map/all_to_all | solution.py:125
  55.7 30.0 %copy-start.2 = (bf16[1,512,2048]{2,1,0:T(8,128)(2,1)S(1)}, bf16[1,512,2048]{2,1,0:T(8,128)(2,1)}, u32[]{:S(2)}) copy-start(bf16[1,512,2048]{2,1,0:T(8,128)(2,1)} %param.17) | copy-start | bytes 6291460
  56.5 14.2 %all-to-all-start.2 = ((f32[32,2,768]{2,1,0:T(2,128)}), f32[32,2,768]{2,1,0:T(2,128)S(1)}, u32[]{:S(2)}, u32[]{:S(2)}) async-start(f32[32,2,768]{2,1,0:T(2,128)} %reshape.266), calls=%async_computation.2 | async-start | bytes 393216 | tf_op jit(solution)/shard_map/all_to_all | solution.py:138
  71.4 14.8 %copy-start.5 = (bf16[2,128]{1,0:T(2,128)(2,1)}, bf16[2,128]{1,0:T(2,128)(2,1)S(1)}, u32[]{:S(2)}) copy-start(bf16[2,128]{1,0:T(2,128)(2,1)S(1)} %get-tuple-element.19) | copy-start | bytes 1540
Sparse Core Ops, SparseCore 0:
  10.4 63.6 all-gather.10
  76.4 60.2 all-gather.12
  139.1 170.4 all-gather.8
  311.2 171.8 all-gather.14
